TPU v7x, 128 devices: a 2x2x16 block of a 8x8x16 slice. The times are simulated.
128 devices in a mesh: groups: 4 (over x, y), wide: 32 (over z, core).
Axes of the slice: x: 2, y: 2, z: 16, core: 2. Of those that a mesh axis runs over, the one named last changes fastest.
The devices are a block of a 8x8x16 slice.
Arguments:
- half_integrals: float32 [1024, 512, 800], P(('groups', 'wide')), parts along dimension 0, may hold values from -40 to 40
- pair_list: int32 [1024, 2], P('groups'), parts along dimension 0, may hold values from 0 to 199, as said below
- occupied_energy: float32 [800], P('groups'), parts along dimension 0, may hold values from -3 to -0.3
- virtual_orbitals: float32 [3200, 600], P('groups'), parts along dimension 0, may hold values from -0.21875 to 0.21875
- tile_order: int32 [64], replicated, may hold values from 0 to 63, each once
Outputs:
- transformed: float32 [1024, 512, 600], P('groups', 'wide'), parts along dimension 0
- pair_rms: float32 [1024], P('groups'), parts along dimension 0
There are 4 independent parts, one for each index of `groups`. A program takes and returns all parts, laid end to end along the dimension named above; an argument that names none is the same for every part. Nothing has to cross between parts.
Inputs may be any that keep to these rules, and one draw needn't show every extreme that they name: `pair_list`: each row is a distinct pair (i, j) with i <= j.
All inputs are finite; a program needn't handle non-finite values.
Results may differ from a plain program's by a relative error of at most 0.00007.
Values sent between devices are 32-bit elements; how exact they have to be, the bound alone decides.
No kernel may reach another device: no remote copies, remote signals or barrier semaphores. Data moves between devices by JAX's collectives and lax.ppermute only.
A program may use at most 128 MiB of HBM per device.

v0:
```python
import jax
import jax.numpy as jnp
from jax import lax
from jax.sharding import PartitionSpec as P

TILE_S = 8


def laid_out(blocks, dim):
    blocks = jnp.moveaxis(blocks, 0, dim)
    shape = blocks.shape
    return blocks.reshape(*shape[:dim], shape[dim] * shape[dim + 1], *shape[dim + 2 :])


def copy_for_each(x, axis):
    peers = lax.axis_size(axis)
    return lax.all_to_all(jnp.broadcast_to(x[None], (peers, *x.shape)), axis, 0, 0, tiled=True)


def collect(x, axis, dim):
    return laid_out(copy_for_each(x, axis), dim)


def pair_weights(pair_list, occupied_energy):
    orbital = jnp.arange(occupied_energy.shape[0], dtype=jnp.int32)
    first = jnp.sum(
        jnp.where(pair_list[:, 0:1] == orbital[None, :], occupied_energy[None, :], 0.0), axis=1
    )
    second = jnp.sum(
        jnp.where(pair_list[:, 1:2] == orbital[None, :], occupied_energy[None, :], 0.0), axis=1
    )
    return jnp.exp(0.3 * (first + second))


def transform(block, virtual_orbitals, scale):
    product = jnp.einsum("psr,ra->psa", block, virtual_orbitals, precision=lax.Precision.HIGHEST)
    return product * scale[:, None, None]


def shards(half_integrals, pair_list, occupied_energy, virtual_orbitals, tile_order):
    pair_rows = half_integrals.shape[0]
    columns = half_integrals.shape[1]
    basis = half_integrals.shape[2]
    virtuals = virtual_orbitals.shape[1]
    weights = pair_weights(pair_list, occupied_energy)
    tiled = half_integrals.reshape(pair_rows, tile_order.shape[0], TILE_S, basis)
    ordered = jnp.take(tiled, tile_order, axis=1).reshape(pair_rows, columns, basis)
    own_weights = lax.dynamic_slice_in_dim(weights, lax.axis_index("wide") * pair_rows, pair_rows)
    local = transform(ordered, virtual_orbitals, own_weights)
    squares = jnp.sum(local * local, axis=(1, 2))
    transformed = lax.all_to_all(local, "wide", split_axis=1, concat_axis=0, tiled=True)
    totals = collect(squares, "wide", 0)
    pair_rms = jnp.sqrt(totals / (columns * virtuals) + 1e-06)
    return (transformed, pair_rms)


def solution(mesh):
    in_specs = (
        P(("groups", "wide"), None, None),
        P("groups", None),
        P("groups"),
        P("groups", None),
        P(),
    )
    out_specs = (P("groups", "wide", None), P("groups"))
    return jax.shard_map(shards, mesh=mesh, in_specs=in_specs, out_specs=out_specs, check_vma=False)
```

profile of v0, /device:TPU:196, one launch (start us, length us, event | category | flops | bytes accessed | tf_op | source)
XLA Modules:
  0.0 601.8 jit_solution(2941339736911717177)
XLA Ops:
  0.6 0.0 copy-start
  0.6 0.8 compare_select_fusion
  1.5 0.7 compare_and_fusion
  2.1 0.8 fusion.6
  2.9 15.6 %copy.23 = f32[8,512,800]{2,1,0:T(8,128)} copy(f32[8,512,800]{1,2,0:T(8,128)} %param.5) | data formatting | bytes 26214400 | tf_op args[0]
  18.4 0.0 copy-start.2
  18.4 12.4 %copy.24 = f32[8,64,8,800]{3,2,0,1:T(8,128)} copy(f32[8,64,8,800]{3,2,1,0:T(8,128)} %bitcast.23) | data formatting | bytes 26214400 | tf_op jit(solution)/shard_map/reshape | solution.py:46
  30.8 0.1 broadcast_in_dim.43
  30.9 0.1 broadcast_in_dim.44
  31.0 0.0 copy-done.2
  31.0 0.1 select_reduce_fusion
  31.2 0.1 dynamic_slice.3
  31.2 11.9 %gather_fusion = f32[64,8,8,800]{3,2,1,0:T(8,128)} fusion(f32[8,64,8,800]{3,2,0,1:T(8,128)} %copy.24, s32[1024]{0:T(1024)S(1)} %pad_clamp_fusion), kind=kCustom, calls=%fused_computation | custom fusion | bytes 26214656 | tf_op jit(solution)/shard_map/jit(_take)/gather | solution.py:47
  43.1 0.0 copy-done
  43.1 37.2 %multiply_reduce_fusion = (f32[8]{0:T(128)S(1)}, f32[8,512,600]{1,2,0:T(8,128)}) fusion(f32[8]{0:T(128)S(1)} %dynamic_slice.3, f32[800,600]{1,0:T(8,128)S(1)} %copy-done, pred[512]{0:T(512)(128)(4,1)S(1)} %broadcast_in_dim.44, f32[64,8,8,800]{3,2,1,0:T(8,128)} %gather_fusion), kind=kOutput, calls=%fused_computation.4 | convolution fusion | flops 23603609600 | bytes 24858176 | tf_op jit(solution)/shard_map/psr,ra->psa/dot_general | solution.py:36
  80.3 0.6 broadcast_in_dim.50
  80.9 17.0 %all-to-all-start.1 = ((f32[32,1,8]{2,1,0:T(1,128)}), f32[32,1,8]{2,1,0:T(1,128)S(1)}, u32[]{:S(2)}, u32[]{:S(2)}) async-start(f32[32,1,8]{2,1,0:T(1,128)} %broadcast_in_dim.50), calls=%async_computation.1 | async-start | bytes 32768 | tf_op jit(solution)/shard_map/all_to_all | solution.py:17
  98.0 12.3 %copy.27 = f32[8,512,600]{2,0,1:T(8,128)} copy(f32[8,512,600]{1,2,0:T(8,128)} %get-tuple-element.13) | data formatting | bytes 19660800 | tf_op jit(solution)/shard_map/mul | solution.py:37
  110.2 0.0 all-to-all-done.1
  110.2 12.4 %all-to-all-start = ((f32[8,512,600]{2,0,1:T(8,128)}), f32[8,512,600]{2,0,1:T(8,128)}, u32[]{:S(2)}, u32[]{:S(2)}) async-start(f32[8,512,600]{2,0,1:T(8,128)} %copy.27), calls=%async_computation | async-start | bytes 20971520 | tf_op jit(solution)/shard_map/all_to_all | solution.py:51
  122.7 0.1 sqrt_reduce_fusion
  122.8 0.7 sqrt.7
  123.4 457.5 %all-to-all-done = f32[8,512,600]{2,0,1:T(8,128)} async-done(((f32[8,512,600]{2,0,1:T(8,128)}), f32[8,512,600]{2,0,1:T(8,128)}, u32[]{:S(2)}, u32[]{:S(2)}) %all-to-all-start) | async-done | bytes 9830432 | tf_op jit(solution)/shard_map/all_to_all | solution.py:51
  580.9 0.0 copy-start.1
  580.9 9.8 %copy.29 = f32[32,8,16,600]{3,2,1,0:T(8,128)} copy(f32[32,8,16,600]{3,1,2,0:T(8,128)} %bitcast.8) | data formatting | bytes 19660800 | tf_op jit(solution)/shard_map/all_to_all | solution.py:51
  590.8 11.0 %copy.30 = f32[256,16,600]{0,2,1:T(8,128)} copy(f32[256,16,600]{2,1,0:T(8,128)} %bitcast.24) | data formatting | bytes 19660800
  601.8 0.0 copy-done.1
  (2 shorter events, 0.0 us)
Async XLA Ops:
  0.6 42.5 %copy-start = (f32[800,600]{1,0:T(8,128)S(1)}, f32[800,600]{1,0:T(8,128)}, u32[]{:S(2)}) copy-start(f32[800,600]{1,0:T(8,128)} %param.8) | copy-start | bytes 5760004
  18.4 12.6 %copy-start.2 = (f32[200]{0:T(256)S(1)}, f32[200]{0:T(256)}, u32[]{:S(2)}) copy-start(f32[200]{0:T(256)} %param.7) | copy-start | bytes 2404
  80.9 29.3 %all-to-all-start.1 = ((f32[32,1,8]{2,1,0:T(1,128)}), f32[32,1,8]{2,1,0:T(1,128)S(1)}, u32[]{:S(2)}, u32[]{:S(2)}) async-start(f32[32,1,8]{2,1,0:T(1,128)} %broadcast_in_dim.50), calls=%async_computation.1 | async-start | bytes 32768 | tf_op jit(solution)/shard_map/all_to_all | solution.py:17
  110.2 470.7 %all-to-all-start = ((f32[8,512,600]{2,0,1:T(8,128)}), f32[8,512,600]{2,0,1:T(8,128)}, u32[]{:S(2)}, u32[]{:S(2)}) async-start(f32[8,512,600]{2,0,1:T(8,128)} %copy.27), calls=%async_computation | async-start | bytes 20971520 | tf_op jit(solution)/shard_map/all_to_all | solution.py:51
  580.9 20.8 %copy-start.1 = (f32[800,600]{1,0:T(8,128)S(1)}, f32[800,600]{1,0:T(8,128)}, u32[]{:S(2)}) copy-start(f32[800,600]{1,0:T(8,128)} %param.8) | copy-start | bytes 5760004
where the time goes:
time: 603 us; the launch traced here: 602 us
  waiting for transfers between devices  458 us (76%)
  local copies, waits for them, and re-layouts  75.2 us (12%)
  matrix products  37.2 us (6%)
  starting transfers between devices  29.4 us (5%)
    all_to_all x1, waiting for transfers between devices, shards(): lax.all_to_all(local, 'wide', split_axis=1, concat_axis=0, tiled=True)  458 us
    dot_general x1, matrix products, transform(): jnp.einsum('psr,ra->psa', block, virtual_orbitals, precision=lax.Precisio...  37.2 us
    unnamed x8, local copies, waits for them, and re-layouts  26.6 us
    all_to_all x1, starting transfers between devices, copy_for_each(): lax.all_to_all(jnp.broadcast_to(x[None], (peers, *x.shape)), axis, 0, 0,...  17 us
    all_to_all x1, starting transfers between devices, shards(): lax.all_to_all(local, 'wide', split_axis=1, concat_axis=0, tiled=True)  12.4 us
    reshape x1, local copies, waits for them, and re-layouts, shards(): half_integrals.reshape(pair_rows, tile_order.shape[0], TILE_S, basis)  12.4 us
    mul x1, local copies, waits for them, and re-layouts, transform(): return product * scale[:, None, None]  12.3 us
  transfers between devices with their start and end apart: 2, of which 1 were waited for; matrix products, arithmetic and copies ran while one was open for 2% of the time, Pallas kernels for 0%

commit v1 on v0

v1 whole, which is shorter than its diff:
```python
import functools

import jax
import jax.numpy as jnp
from jax import lax
from jax.experimental import pallas as pl
from jax.experimental.pallas import tpu as pltpu
from jax.sharding import PartitionSpec as P


TILE_S = 8
LANES = 128
CHUNKS = 5
GATHER_ROWS = 80
STEP = 40
PACK = 280
UNPACK = 80
LAST = 40
EARLY = (2, 2)


SMEM = pl.BlockSpec(memory_space=pltpu.SMEM)
VMEM = pl.BlockSpec(memory_space=pltpu.VMEM)
ANY = pl.BlockSpec(memory_space=pl.ANY)


def pair_weights(pair_list, occupied_energy):
    orbital = jnp.arange(occupied_energy.shape[0], dtype=jnp.int32)
    first = jnp.sum(
        jnp.where(pair_list[:, 0:1] == orbital[None, :], occupied_energy[None, :], 0.0), axis=1
    )
    second = jnp.sum(
        jnp.where(pair_list[:, 1:2] == orbital[None, :], occupied_energy[None, :], 0.0), axis=1
    )
    return jnp.exp(0.3 * (first + second))


def split(x):
    high = x.astype(jnp.bfloat16)
    return high, (x - high.astype(jnp.float32)).astype(jnp.bfloat16)


def product_of(v_high, v_low, high, low):
    dot = functools.partial(jnp.dot, preferred_element_type=jnp.float32)
    return dot(v_high, low) + dot(v_low, high) + dot(v_high, high)


def paired_order(rows, pairs):
    lane = lax.broadcasted_iota(jnp.int32, (rows, LANES), 1)
    half = pairs * TILE_S
    return (lane // half) * half + (lane % pairs) * TILE_S + (lane // pairs) % TILE_S


def take_lanes(x, index):
    return jnp.take_along_axis(x, index, axis=1, mode="promise_in_bounds")


def early_kernel(shifts, peers, first, pos, order, half, *refs):
    n = len(shifts)
    if first:
        orbitals, refs = refs[0], refs[1:]
        outs, (v_high, v_low) = refs[:n], refs[n : n + 2]
        data, high, low, sems = refs[n + 2 :]
    else:
        v_high, v_low = refs[:2]
        outs = refs[2 : n + 2]
        data, high, low, sems = refs[n + 2 :]
    pairs, basis, _ = data.shape
    rows_out = outs[0].shape[0]
    span = basis // CHUNKS
    copies = [
        pltpu.make_async_copy(
            half.at[:, pl.ds(c * span, span), :], data.at[:, pl.ds(c * span, span), :], sems.at[c]
        )
        for c in range(CHUNKS)
    ]
    for copy in copies:
        copy.start()
    if first:
        v_high[...], v_low[...] = split(orbitals[...].T)
    group = lax.broadcasted_iota(jnp.int32, (GATHER_ROWS, LANES), 1) // TILE_S
    index = paired_order(GATHER_ROWS, pairs)
    per_block = LANES // TILE_S
    sources = []
    for shift in shifts:
        owner = lax.rem(pos[0] + shift, peers)
        for h in range(2):
            tile = order[2 * owner + h]
            start = pl.multiple_of((tile // per_block) * LANES, LANES)
            sources.append((start, h * pairs, lax.rem(tile, per_block)))

    def gather(step, carry):
        rows = pl.ds(pl.multiple_of(step * GATHER_ROWS, GATHER_ROWS), GATHER_ROWS)
        for n in range(len(shifts)):
            block = None
            for start, base, place in sources[2 * n : 2 * n + 2]:
                for p in range(pairs):
                    amount = lax.rem((base + p - place + per_block) * TILE_S, LANES)
                    x = pltpu.roll(data[p, rows, pl.ds(start, LANES)], amount, 1)
                    block = x if block is None else jnp.where(group == base + p, x, block)
            columns = pl.ds(n * LANES, LANES)
            high[rows, columns], low[rows, columns] = split(take_lanes(block, index))
        return carry

    for c in range(CHUNKS):
        copies[c].wait()
        lax.fori_loop(c * span // GATHER_ROWS, (c + 1) * span // GATHER_ROWS, gather, 0)
    product = product_of(v_high[:rows_out], v_low[:rows_out], high[...], low[...])
    for m in range(n):
        outs[m][...] = product[:, m * LANES : (m + 1) * LANES]


def early_blocks(shifts, peers, cut, pos, order, half, *orbitals):
    pairs, basis, columns = half.shape
    first = len(orbitals) == 1
    virtuals = orbitals[0].shape[1 if first else 0]
    n = len(shifts)
    more = [jax.ShapeDtypeStruct((virtuals, basis), jnp.bfloat16)] * 2 if first else []
    return pl.pallas_call(
        functools.partial(early_kernel, shifts, peers, first),
        in_specs=[SMEM, SMEM, ANY] + [VMEM] * len(orbitals),
        out_specs=[VMEM] * (n + len(more)),
        out_shape=[jax.ShapeDtypeStruct((cut, LANES), jnp.float32)] * n + more,
        scratch_shapes=[
            pltpu.VMEM((pairs, basis, columns), jnp.float32),
            pltpu.VMEM((basis, n * LANES), jnp.bfloat16),
            pltpu.VMEM((basis, n * LANES), jnp.bfloat16),
            pltpu.SemaphoreType.DMA((CHUNKS,)),
        ],
        cost_estimate=pl.CostEstimate(
            flops=6 * n * LANES * basis * virtuals,
            bytes_accessed=4 * pairs * basis * columns,
            transcendentals=0,
        ),
    )(pos, order, half, *orbitals)


def rest_kernel(shifts, peers, skipped, pos, order, half, v_high, v_low, *refs):
    n = len(shifts) - skipped
    outs = refs[:n]
    ends, squares, products, tiles = refs[n:]
    pairs, virtuals, columns = products.shape
    steps = (virtuals - LAST) // PACK
    step = pl.program_id(0)
    blocks = columns // LANES
    per_block = LANES // TILE_S

    @pl.when(step < pairs)
    def _():
        high, low = split(half[0])
        product = product_of(v_high[...], v_low[...], high, low)
        products[step] = product
        sums = jnp.sum((product * product).reshape(virtuals // 8, 8, columns), axis=0)
        total = sums[:, :LANES]
        for b in range(1, blocks):
            total = total + sums[:, b * LANES : (b + 1) * LANES]
        squares[0] = total

    group = lax.broadcasted_iota(jnp.int32, (STEP, LANES), 1) // TILE_S
    index = paired_order(STEP, pairs)
    front = group < pairs

    def source(owner, h):
        tile = order[2 * owner + h]
        within = lax.rem(tile, per_block)
        place = (tile // per_block) * pairs + lax.rem(within, pairs)
        return place, lax.rem(within // pairs + h, 2) * (LANES // 2)

    def block_for(owner):
        a, turn_a = source(owner, 0)
        c, turn_c = source(owner, 1)
        return jnp.where(front, pltpu.roll(tiles[a], turn_a, 1), pltpu.roll(tiles[c], turn_c, 1))

    def fill(row):
        rows_in = pl.ds(pl.multiple_of(row, 8), STEP)

        def one(b, carry):
            columns_in = pl.ds(pl.multiple_of(b * LANES, LANES), LANES)
            x = [products[p, rows_in, columns_in] for p in range(pairs)]
            m = 1
            while m < pairs:
                upper = (group & m) != 0
                y = list(x)
                for p in range(pairs):
                    if not p & m:
                        q = p | m
                        y[p] = jnp.where(upper, pltpu.roll(x[q], TILE_S * m, 1), x[p])
                        y[q] = jnp.where(upper, x[q], pltpu.roll(x[p], LANES - TILE_S * m, 1))
                x = y
                m *= 2
            for p in range(pairs):
                tiles[b * pairs + p] = take_lanes(x[p], index)
            return carry

        lax.fori_loop(0, blocks, one, 0)

    @pl.when((step >= pairs) & (step < pairs + steps))
    def _():
        def one(i, carry):
            fill((step - pairs) * PACK + i * STEP)
            rows_out = pl.ds(pl.multiple_of(i * STEP, 8), STEP)
            for j, shift in enumerate(shifts[skipped:]):
                outs[j][rows_out, :] = block_for(lax.rem(pos[0] + shift, peers))
            return carry

        lax.fori_loop(0, PACK // STEP, one, 0)

    @pl.when(step == pairs + steps)
    def _():
        fill(virtuals - LAST)

        def one(owner, carry):
            ends[owner] = block_for(owner)
            return carry

        lax.fori_loop(0, peers, one, 0)


def rest_blocks(shifts, peers, skipped, pos, order, half, v_high, v_low):
    pairs, basis, columns = half.shape
    virtuals = v_high.shape[0]
    n = len(shifts) - skipped
    cut = virtuals - LAST
    steps = cut // PACK
    results = pl.pallas_call(
        functools.partial(rest_kernel, shifts, peers, skipped),
        grid=(pairs + steps + 1,),
        in_specs=[
            SMEM,
            SMEM,
            pl.BlockSpec((1, basis, columns), lambda i: (jnp.minimum(i, pairs - 1), 0, 0)),
        ]
        + [pl.BlockSpec((virtuals, basis), lambda i: (0, 0))] * 2,
        out_specs=[pl.BlockSpec((PACK, LANES), lambda i: (jnp.clip(i - pairs, 0, steps - 1), 0))] * n
        + [
            pl.BlockSpec((peers, LAST, LANES), lambda i: (0, 0, 0)),
            pl.BlockSpec((1, 8, LANES), lambda i: (jnp.minimum(i, pairs - 1), 0, 0)),
        ],
        out_shape=[jax.ShapeDtypeStruct((cut, LANES), jnp.float32)] * n
        + [
            jax.ShapeDtypeStruct((peers, LAST, LANES), jnp.float32),
            jax.ShapeDtypeStruct((pairs, 8, LANES), jnp.float32),
        ],
        scratch_shapes=[
            pltpu.VMEM((pairs, virtuals, columns), jnp.float32),
            pltpu.VMEM((columns * pairs // LANES, STEP, LANES), jnp.float32),
        ],
        cost_estimate=pl.CostEstimate(
            flops=6 * pairs * columns * basis * virtuals,
            bytes_accessed=4 * pairs * basis * columns,
            transcendentals=0,
        ),
        name="rest_blocks",
    )(pos, order, half, v_high, v_low)
    return results[:n], results[n], results[n + 1]


def regroup(x, pairs, upper_of):
    m = 1
    while m < len(x):
        upper = upper_of(m)
        y = list(x)
        for i in range(len(x)):
            if not i & m:
                j = i | m
                y[i] = jnp.where(upper, pltpu.roll(x[j], pairs * m, 1), x[i])
                y[j] = jnp.where(upper, x[j], pltpu.roll(x[i], LANES - pairs * m, 1))
        x = y
        m *= 2
    return x


def unpack_kernel(peers, pairs, pos, weights, *refs):
    ins, out = refs[:peers], refs[-1]
    per = LANES // pairs
    group = lax.broadcasted_iota(jnp.int32, (STEP, LANES), 1) // pairs
    shift = pos[0] * pairs
    inner = lax.rem(shift, LANES)
    outer = lax.div(shift, LANES)
    wrapped = group * pairs < inner
    count = peers // per

    def tile(step, carry):
        rows = pl.ds(pl.multiple_of(step * STEP, 8), STEP)
        halves = [
            regroup(
                [ins[b * per + j][rows, :] for j in range(per)], pairs, lambda m: (group & m) != 0
            )
            for b in range(count)
        ]
        for k in range(per):
            rolled = [pltpu.roll(halves[b][k], inner, 1) for b in range(count)]
            for b in range(count):
                place = pl.multiple_of(lax.rem(b + outer, count) * LANES, LANES)
                value = jnp.where(wrapped, rolled[b - 1], rolled[b])
                out[k, rows, pl.ds(place, LANES)] = value * weights[:, pl.ds(place, LANES)]
        return carry

    lax.fori_loop(0, out.shape[1] // STEP, tile, 0)


def unpack(blocks, pos, weights, pairs, virtuals):
    peers = len(blocks)
    per = LANES // pairs
    total = weights.shape[1]
    return pl.pallas_call(
        functools.partial(unpack_kernel, peers, pairs),
        grid=(blocks[0].shape[0] // UNPACK,),
        in_specs=[SMEM, pl.BlockSpec((1, total), lambda i: (0, 0))]
        + [pl.BlockSpec((UNPACK, LANES), lambda i: (i, 0))] * peers,
        out_specs=pl.BlockSpec((per, UNPACK, total), lambda i: (0, i, 0)),
        out_shape=jax.ShapeDtypeStruct((per, virtuals, total), jnp.float32),
        name="unpack",
    )(pos, weights, *blocks)


def unpack_last_kernel(pairs, weights, ends, _, out):
    peers, rows, _ = ends.shape
    per = LANES // pairs
    group = lax.broadcasted_iota(jnp.int32, (rows, LANES), 1) // pairs
    for b in range(peers // per):
        lanes = pl.ds(b * LANES, LANES)
        done = regroup(
            [ends[b * per + j] for j in range(per)], pairs, lambda m: (group & m) != 0
        )
        for k in range(per):
            out[k, :, lanes] = done[k] * weights[:, lanes]


def unpack_last(ends, weights, pairs, into):
    per, virtuals, total = into.shape
    rows = ends.shape[1]
    return pl.pallas_call(
        functools.partial(unpack_last_kernel, pairs),
        grid=(1,),
        in_specs=[
            pl.BlockSpec((1, total), lambda i: (0, 0)),
            pl.BlockSpec(ends.shape, lambda i: (0, 0, 0)),
            ANY,
        ],
        out_specs=pl.BlockSpec((per, rows, total), lambda i: (0, virtuals // rows - 1, 0)),
        out_shape=jax.ShapeDtypeStruct(into.shape, into.dtype),
        input_output_aliases={2: 0},
        name="unpack_last",
    )(weights, ends, into)


def order_of_shifts(peers):
    far = []
    for d in range(peers // 2 - 1, 0, -1):
        far += [d, peers - d]
    far.insert(sum(EARLY), peers // 2)
    return far + [0]


def shards(half_integrals, pair_list, occupied_energy, virtual_orbitals, tile_order):
    pairs, columns, _ = half_integrals.shape
    virtuals = virtual_orbitals.shape[1]
    peers = lax.axis_size("wide")
    cut = virtuals - LAST
    pos = lax.axis_index("wide").astype(jnp.int32).reshape(1)
    half = jnp.swapaxes(half_integrals, 1, 2)
    shifts = tuple(order_of_shifts(peers))
    blocks = []
    kept = [virtual_orbitals]
    at = 0
    for n in EARLY:
        results = early_blocks(shifts[at : at + n], peers, cut, pos, tile_order, half, *kept)
        blocks += results[:n]
        kept = results[n:] or kept
        at += n
    more, ends, sums = rest_blocks(shifts, peers, at, pos, tile_order, half, *kept)
    blocks += more
    arrived = {}
    for n, s in enumerate(shifts):
        block = blocks[n]
        if s:
            block = lax.ppermute(block, "wide", [(i, (i + s) % peers) for i in range(peers)])
        arrived[(peers - s) % peers] = block
    squares = jnp.sum(sums, axis=(1, 2))
    sent = jnp.broadcast_to(squares[None, None], (peers, 1, pairs))
    totals = lax.all_to_all(sent, "wide", 0, 0, tiled=True).reshape(peers * pairs)
    ends = lax.all_to_all(ends, "wide", 0, 0, tiled=True)
    weights = pair_weights(pair_list, occupied_energy)
    pair_rms = jnp.sqrt(totals * weights * weights / (columns * virtuals) + 1e-06)
    out = unpack([arrived[i] for i in range(peers)], pos, weights[None], pairs, virtuals)
    out = unpack_last(ends, weights[None], pairs, out)
    return (jnp.transpose(out, (2, 0, 1)), pair_rms)


def solution(mesh):
    in_specs = (
        P(("groups", "wide"), None, None),
        P("groups", None),
        P("groups"),
        P("groups", None),
        P(),
    )
    out_specs = (P("groups", "wide", None), P("groups"))
    return jax.shard_map(shards, mesh=mesh, in_specs=in_specs, out_specs=out_specs, check_vma=False)
```

time: 603 us -> 706 us (1.17)
  starting transfers between devices: 29.4 us -> 204 us
  Pallas kernels: 0 us -> 100 us
  waiting for transfers between devices: 458 us -> 368 us
  local copies, waits for them, and re-layouts: 75.2 us -> 1.53 us
  matrix products: 37.2 us -> 0 us
  blocking collectives: 0 us -> 27.8 us
    all_to_all x2 -> x1, waiting for transfers between devices: 458 us -> 0.01 us  [shards(): ends = lax.all_to_all(ends, 'wide', 0, 0, tiled=True)]
    ppermute x0 -> x31, waiting for transfers between devices: none -> 368 us  [shards(): lax.ppermute(block, 'wide', [(i, (i + s) % peers) for i in range(peers)])]
    ppermute x0 -> x31, starting transfers between devices: none -> 198 us  [shards(): lax.ppermute(block, 'wide', [(i, (i + s) % peers) for i in range(peers)])]
    pallas_call x0 -> x5, Pallas kernels: none -> 100 us  [the longest x1 58.7 us: rest_blocks(): pl.pallas_call(functools.partial(rest_kernel, shifts, peers, skipped), gr...]
    dot_general x1 -> x0, matrix products: 37.2 us -> none  [transform(): jnp.einsum('psr,ra->psa', block, virtual_orbitals, precision=lax.Precisio...]
    all_to_all x0 -> x1, blocking collectives: none -> 27.8 us  [shards(): lax.all_to_all(sent, 'wide', 0, 0, tiled=True).reshape(peers * pairs)]
    unnamed x8 -> x32, local copies, waits for them, and re-layouts: 26.6 us -> 0.89 us
    all_to_all x2 -> x1, starting transfers between devices: 29.4 us -> 5.28 us  [shards(): ends = lax.all_to_all(ends, 'wide', 0, 0, tiled=True)]
  transfers between devices with their start and end apart: 2 -> 32, of which waited for: 1 -> 23; matrix products, arithmetic and copies ran while one was open for 2% -> 0% of each run, Pallas kernels for 0% -> 4%
where the time goes in v1:
time: 706 us; the launch traced here: 705 us
  waiting for transfers between devices  368 us (52%)
  starting transfers between devices  204 us (29%)
  Pallas kernels  100 us (14%)
  blocking collectives  27.8 us (4%)
    ppermute x31, waiting for transfers between devices, shards(): lax.ppermute(block, 'wide', [(i, (i + s) % peers) for i in range(peers)])  368 us
    ppermute x31, starting transfers between devices, shards(): lax.ppermute(block, 'wide', [(i, (i + s) % peers) for i in range(peers)])  198 us
    pallas_call x1, Pallas kernels, rest_blocks(): pl.pallas_call(functools.partial(rest_kernel, shifts, peers, skipped), gr...  58.7 us
    all_to_all x1, blocking collectives, shards(): lax.all_to_all(sent, 'wide', 0, 0, tiled=True).reshape(peers * pairs)  27.8 us
    pallas_call x2, Pallas kernels, early_blocks(): pl.pallas_call(functools.partial(early_kernel, shifts, peers, first), in_...  21.8 us
    pallas_call x1, Pallas kernels, unpack(): pl.pallas_call(functools.partial(unpack_kernel, peers, pairs), grid=(bloc...  16.8 us
  transfers between devices with their start and end apart: 32, of which 23 were waited for; matrix products, arithmetic and copies ran while one was open for 0% of the time, Pallas kernels for 4%

profile of v1, /device:TPU:196, one launch (start us, length us, event | category | flops | bytes accessed | tf_op | source)
XLA Modules:
  0.0 705.3 jit_solution(7303199777535209578)
XLA Ops:
  0.6 11.1 %shard_map.68 = (f32[560,128]{1,0:T(8,128)}, f32[560,128]{1,0:T(8,128)}, bf16[600,800]{1,0:T(8,128)(2,1)}, bf16[600,800]{1,0:T(8,128)(2,1)}) custom-call(s32[1]{0:T(128)} %bitcast.3.pos, s32[64]{0:T(128)} %order.5, f32[8,800,512]{2,1,0:T(8,128)} %bitcast.6, f32[800,600]{1,0:T(8,128)} %refs_0_.1), custom_call_target="tpu_custom_call" | custom-call | flops 737280000 | bytes 13107200 | tf_op jit(solution)/shard_map/pallas_call | solution.py:119
  11.8 58.7 %rest_blocks.1 = (f32[560,128]{1,0:T(8,128)}, f32[560,128]{1,0:T(8,128)}, f32[560,128]{1,0:T(8,128)}, f32[560,128]{1,0:T(8,128)}, f32[560,128]{1,0:T(8,128)}, /*...) custom-call(s32[1]{0:T(128)} %bitcast.3.pos, ...), custom_call_target="tpu_custom_call" | custom-call | flops 11796480000 | bytes 13107200 | tf_op jit(solution)/shard_map/rest_blocks/pallas_call | solution.py:225
  71.5 27.8 %all_to_all.10 = f32[32,1,8]{2,1,0:T(1,128)S(1)} all-to-all(f32[32,1,8]{2,1,0:T(1,128)S(1)} %broadcast_in_dim.30), channel_id=1, replica_groups=mesh['groups'=4,'wide'=32] {'wide'}, dimensions={0} | all-to-all | bytes 2048 | tf_op jit(solution)/shard_map/all_to_all | solution.py:382
  104.6 9.4 %collective-permute-start.14 = (f32[560,128]{1,0:T(8,128)S(1)}, f32[560,128]{1,0:T(8,128)S(1)}, u32[]{:S(2)}, u32[]{:S(2)}) collective-permute-start(f32[560,128]{1,0:T(8,128)S(1)} %copy-done.15), channel_id=1, source_target_pairs={{0,17},{1,18},{2,19},{3,20},{4,21},{5,22},{6,23},{7,24},{8,25},{9,... | collective-permute-start | bytes 860168 | tf_op jit(solution)/shard_map/ppermute | solution.py:378
  114.3 10.7 %shard_map.69 = (f32[560,128]{1,0:T(8,128)}, f32[560,128]{1,0:T(8,128)}) custom-call(s32[1]{0:T(128)} %bitcast.3.pos, s32[64]{0:T(128)} %order.5, f32[8,800,512]{2,1,0:T(8,128)} %bitcast.8, bf16[600,800]{1,0:T(8,128)(2,1)} %get-tuple-element.38.v_high.refs_0_, bf16[600,800]{1,0:T(8,128)(2,1)} %get-tuple-element.39.v_low.refs_1_), custom_call_target="tpu_custom_call" | custom-call | flops 737280000 | bytes 13107200 | tf_op jit(solution)/shard_map/pallas_call | solution.py:119
  125.0 8.8 %collective-permute-start.13 = (f32[560,128]{1,0:T(8,128)}, f32[560,128]{1,0:T(8,128)S(1)}, u32[]{:S(2)}, u32[]{:S(2)}) collective-permute-start(f32[560,128]{1,0:T(8,128)} %get-tuple-element.55), channel_id=1, source_target_pairs={{0,18},{1,19},{2,20},{3,21},{4,22},{5,23},{6,24},{7,25},{8,26},{9,... | collective-permute-start | bytes 860168 | tf_op jit(solution)/shard_map/ppermute | solution.py:378
  135.6 71.6 %collective-permute-done.14.refs_15_ = f32[560,128]{1,0:T(8,128)S(1)} collective-permute-done((f32[560,128]{1,0:T(8,128)S(1)}, f32[560,128]{1,0:T(8,128)S(1)}, u32[]{:S(2)}, u32[]{:S(2)}) %collective-permute-start.14) | collective-permute-done | bytes 286752 | tf_op jit(solution)/shard_map/ppermute | solution.py:378
  212.8 8.1 %collective-permute-done.17.refs_18_ = f32[560,128]{1,0:T(8,128)S(1)} collective-permute-done((f32[560,128]{1,0:T(8,128)}, f32[560,128]{1,0:T(8,128)S(1)}, u32[]{:S(2)}, u32[]{:S(2)}) %collective-permute-start.17) | collective-permute-done | bytes 286752 | tf_op jit(solution)/shard_map/ppermute | solution.py:378
  220.9 11.2 %collective-permute-start.4 = (f32[560,128]{1,0:T(8,128)}, f32[560,128]{1,0:T(8,128)S(1)}, u32[]{:S(2)}, u32[]{:S(2)}) collective-permute-start(f32[560,128]{1,0:T(8,128)} %get-tuple-element.46), channel_id=1, source_target_pairs={{0,27},{1,28},{2,29},{3,30},{4,31},{5,0},{6,1},{7,2},{8,3},{9,4},{... | collective-permute-start | bytes 860168 | tf_op jit(solution)/shard_map/ppermute | solution.py:378
  245.8 7.5 %collective-permute-done.3.refs_4_ = f32[560,128]{1,0:T(8,128)S(1)} collective-permute-done((f32[560,128]{1,0:T(8,128)}, f32[560,128]{1,0:T(8,128)S(1)}, u32[]{:S(2)}, u32[]{:S(2)}) %collective-permute-start.3) | collective-permute-done | bytes 286752 | tf_op jit(solution)/shard_map/ppermute | solution.py:378
  259.5 9.2 %collective-permute-done.4.refs_5_ = f32[560,128]{1,0:T(8,128)S(1)} collective-permute-done((f32[560,128]{1,0:T(8,128)}, f32[560,128]{1,0:T(8,128)S(1)}, u32[]{:S(2)}, u32[]{:S(2)}) %collective-permute-start.4) | collective-permute-done | bytes 286752 | tf_op jit(solution)/shard_map/ppermute | solution.py:378
  268.7 7.9 %collective-permute-start.9 = (f32[560,128]{1,0:T(8,128)}, f32[560,128]{1,0:T(8,128)}, u32[]{:S(2)}, u32[]{:S(2)}) collective-permute-start(f32[560,128]{1,0:T(8,128)} %get-tuple-element.51), channel_id=1, source_target_pairs={{0,22},{1,23},{2,24},{3,25},{4,26},{5,27},{6,28},{7,29},{8,30},{9,... | collective-permute-start | bytes 860168 | tf_op jit(solution)/shard_map/ppermute | solution.py:378
  276.5 10.9 %collective-permute-done.5.refs_6_ = f32[560,128]{1,0:T(8,128)S(1)} collective-permute-done((f32[560,128]{1,0:T(8,128)}, f32[560,128]{1,0:T(8,128)S(1)}, u32[]{:S(2)}, u32[]{:S(2)}) %collective-permute-start.5) | collective-permute-done | bytes 286752 | tf_op jit(solution)/shard_map/ppermute | solution.py:378
  288.6 21.3 %collective-permute-done.6.refs_7_ = f32[560,128]{1,0:T(8,128)} collective-permute-done((f32[560,128]{1,0:T(8,128)}, f32[560,128]{1,0:T(8,128)}, u32[]{:S(2)}, u32[]{:S(2)}) %collective-permute-start.6) | collective-permute-done | bytes 286752 | tf_op jit(solution)/shard_map/ppermute | solution.py:378
  309.9 8.1 %collective-permute-start.11 = (f32[560,128]{1,0:T(8,128)}, f32[560,128]{1,0:T(8,128)}, u32[]{:S(2)}, u32[]{:S(2)}) collective-permute-start(f32[560,128]{1,0:T(8,128)} %get-tuple-element.53), channel_id=1, source_target_pairs={{0,20},{1,21},{2,22},{3,23},{4,24},{5,25},{6,26},{7,27},{8,28},{9,... | collective-permute-start | bytes 860168 | tf_op jit(solution)/shard_map/ppermute | solution.py:378
  318.0 25.3 %collective-permute-done.7.refs_8_ = f32[560,128]{1,0:T(8,128)} collective-permute-done((f32[560,128]{1,0:T(8,128)}, f32[560,128]{1,0:T(8,128)}, u32[]{:S(2)}, u32[]{:S(2)}) %collective-permute-start.7) | collective-permute-done | bytes 286752 | tf_op jit(solution)/shard_map/ppermute | solution.py:378
  343.4 19.9 %collective-permute-done.8.refs_9_ = f32[560,128]{1,0:T(8,128)} collective-permute-done((f32[560,128]{1,0:T(8,128)}, f32[560,128]{1,0:T(8,128)}, u32[]{:S(2)}, u32[]{:S(2)}) %collective-permute-start.8) | collective-permute-done | bytes 286752 | tf_op jit(solution)/shard_map/ppermute | solution.py:378
  369.2 31.3 %collective-permute-done.9.refs_10_ = f32[560,128]{1,0:T(8,128)} collective-permute-done((f32[560,128]{1,0:T(8,128)}, f32[560,128]{1,0:T(8,128)}, u32[]{:S(2)}, u32[]{:S(2)}) %collective-permute-start.9) | collective-permute-done | bytes 286752 | tf_op jit(solution)/shard_map/ppermute | solution.py:378
  405.4 16.0 %collective-permute-done.10.refs_11_ = f32[560,128]{1,0:T(8,128)} collective-permute-done((f32[560,128]{1,0:T(8,128)}, f32[560,128]{1,0:T(8,128)}, u32[]{:S(2)}, u32[]{:S(2)}) %collective-permute-start.10) | collective-permute-done | bytes 286752 | tf_op jit(solution)/shard_map/ppermute | solution.py:378
  421.4 15.0 %collective-permute-start.19 = (f32[560,128]{1,0:T(8,128)}, f32[560,128]{1,0:T(8,128)}, u32[]{:S(2)}, u32[]{:S(2)}) collective-permute-start(f32[560,128]{1,0:T(8,128)} %get-tuple-element.61), channel_id=1, source_target_pairs={{0,12},{1,13},{2,14},{3,15},{4,16},{5,17},{6,18},{7,19},{8,20},{9,... | collective-permute-start | bytes 860168 | tf_op jit(solution)/shard_map/ppermute | solution.py:378
  436.4 17.3 %collective-permute-done.11.refs_12_ = f32[560,128]{1,0:T(8,128)} collective-permute-done((f32[560,128]{1,0:T(8,128)}, f32[560,128]{1,0:T(8,128)}, u32[]{:S(2)}, u32[]{:S(2)}) %collective-permute-start.11) | collective-permute-done | bytes 286752 | tf_op jit(solution)/shard_map/ppermute | solution.py:378
  453.7 25.7 %collective-permute-start.20 = (f32[560,128]{1,0:T(8,128)}, f32[560,128]{1,0:T(8,128)}, u32[]{:S(2)}, u32[]{:S(2)}) collective-permute-start(f32[560,128]{1,0:T(8,128)} %get-tuple-element.62), channel_id=1, source_target_pairs={{0,11},{1,12},{2,13},{3,14},{4,15},{5,16},{6,17},{7,18},{8,19},{9,... | collective-permute-start | bytes 860168 | tf_op jit(solution)/shard_map/ppermute | solution.py:378
  479.4 25.5 %collective-permute-done.12.refs_13_ = f32[560,128]{1,0:T(8,128)} collective-permute-done((f32[560,128]{1,0:T(8,128)}, f32[560,128]{1,0:T(8,128)}, u32[]{:S(2)}, u32[]{:S(2)}) %collective-permute-start.12) | collective-permute-done | bytes 286752 | tf_op jit(solution)/shard_map/ppermute | solution.py:378
  504.9 8.5 %collective-permute-start.21 = (f32[560,128]{1,0:T(8,128)}, f32[560,128]{1,0:T(8,128)}, u32[]{:S(2)}, u32[]{:S(2)}) collective-permute-start(f32[560,128]{1,0:T(8,128)} %get-tuple-element.63), channel_id=1, source_target_pairs={{0,10},{1,11},{2,12},{3,13},{4,14},{5,15},{6,16},{7,17},{8,18},{9,... | collective-permute-start | bytes 860168 | tf_op jit(solution)/shard_map/ppermute | solution.py:378
  513.5 21.9 %collective-permute-done.15.refs_16_ = f32[560,128]{1,0:T(8,128)} collective-permute-done((f32[560,128]{1,0:T(8,128)}, f32[560,128]{1,0:T(8,128)}, u32[]{:S(2)}, u32[]{:S(2)}) %collective-permute-start.15) | collective-permute-done | bytes 286752 | tf_op jit(solution)/shard_map/ppermute | solution.py:378
  539.8 23.0 %collective-permute-done.21.refs_22_ = f32[560,128]{1,0:T(8,128)} collective-permute-done((f32[560,128]{1,0:T(8,128)}, f32[560,128]{1,0:T(8,128)}, u32[]{:S(2)}, u32[]{:S(2)}) %collective-permute-start.21) | collective-permute-done | bytes 286752 | tf_op jit(solution)/shard_map/ppermute | solution.py:378
  573.8 29.1 %collective-permute-start.27 = (f32[560,128]{1,0:T(8,128)}, f32[560,128]{1,0:T(8,128)}, u32[]{:S(2)}, u32[]{:S(2)}) collective-permute-start(f32[560,128]{1,0:T(8,128)} %get-tuple-element.69), channel_id=1, source_target_pairs={{0,4},{1,5},{2,6},{3,7},{4,8},{5,9},{6,10},{7,11},{8,12},{9,13},{1... | collective-permute-start | bytes 860168 | tf_op jit(solution)/shard_map/ppermute | solution.py:378
  602.9 19.2 %collective-permute-start.28 = (f32[560,128]{1,0:T(8,128)}, f32[560,128]{1,0:T(8,128)}, u32[]{:S(2)}, u32[]{:S(2)}) collective-permute-start(f32[560,128]{1,0:T(8,128)} %get-tuple-element.70), channel_id=1, source_target_pairs={{0,3},{1,4},{2,5},{3,6},{4,7},{5,8},{6,9},{7,10},{8,11},{9,12},{10... | collective-permute-start | bytes 860168 | tf_op jit(solution)/shard_map/ppermute | solution.py:378
  626.4 16.4 %collective-permute-done.25.refs_26_ = f32[560,128]{1,0:T(8,128)} collective-permute-done((f32[560,128]{1,0:T(8,128)}, f32[560,128]{1,0:T(8,128)}, u32[]{:S(2)}, u32[]{:S(2)}) %collective-permute-start.25) | collective-permute-done | bytes 286752 | tf_op jit(solution)/shard_map/ppermute | solution.py:378
  642.8 10.7 %collective-permute-start.30 = (f32[560,128]{1,0:T(8,128)}, f32[560,128]{1,0:T(8,128)}, u32[]{:S(2)}, u32[]{:S(2)}) collective-permute-start(f32[560,128]{1,0:T(8,128)} %get-tuple-element.72), channel_id=1, source_target_pairs={{0,1},{1,2},{2,3},{3,4},{4,5},{5,6},{6,7},{7,8},{8,9},{9,10},{10,1... | collective-permute-start | bytes 860168 | tf_op jit(solution)/shard_map/ppermute | solution.py:378
  669.0 11.7 %collective-permute-done.29.refs_30_ = f32[560,128]{1,0:T(8,128)} collective-permute-done((f32[560,128]{1,0:T(8,128)}, f32[560,128]{1,0:T(8,128)}, u32[]{:S(2)}, u32[]{:S(2)}) %collective-permute-start.29) | collective-permute-done | bytes 286752 | tf_op jit(solution)/shard_map/ppermute | solution.py:378
  685.0 16.8 %unpack.1._ = f32[16,600,256]{2,1,0:T(8,128)} custom-call(s32[1]{0:T(128)} %bitcast.3.pos, f32[1,256]{1,0:T(1,128)} %bitcast.10, f32[560,128]{1,0:T(8,128)} %get-tuple-element.41.refs_0_, f32[560,128]{1,0:T(8,128)} %copy-done.5, f32[560,128]{1,0:T(8,128)} %copy-done.6, f32[560,128]{1,0:T(8,128)} %copy-done.7, f32[560,128]{1,0:T(8,128)} %copy-done.8, ...), custom_call_target="tpu_custom_call" | custom-call | tf_op jit(solution)/shard_map/unpack/pallas_call | solution.py:306
  (78 shorter events, 88.8 us)
Async XLA Ops:
  99.3 602.5 %all-to-all-start = ((f32[32,40,128]{2,1,0:T(8,128)}), f32[32,40,128]{2,1,0:T(8,128)S(1)}, u32[]{:S(2)}, u32[]{:S(2)}) async-start(f32[32,40,128]{2,1,0:T(8,128)} %get-tuple-element.40), calls=%async_computation | async-start | bytes 1310720 | tf_op jit(solution)/shard_map/all_to_all | solution.py:383
  104.6 102.6 %collective-permute-start.14 = (f32[560,128]{1,0:T(8,128)S(1)}, f32[560,128]{1,0:T(8,128)S(1)}, u32[]{:S(2)}, u32[]{:S(2)}) collective-permute-start(f32[560,128]{1,0:T(8,128)S(1)} %copy-done.15), channel_id=1, source_target_pairs={{0,17},{1,18},{2,19},{3,20},{4,21},{5,22},{6,23},{7,24},{8,25},{9,... | collective-permute-start | bytes 860168 | tf_op jit(solution)/shard_map/ppermute | solution.py:378
  114.0 93.2 %collective-permute-start.16 = (f32[560,128]{1,0:T(8,128)S(1)}, f32[560,128]{1,0:T(8,128)S(1)}, u32[]{:S(2)}, u32[]{:S(2)}) collective-permute-start(f32[560,128]{1,0:T(8,128)S(1)} %copy-done.14), channel_id=1, source_target_pairs={{0,15},{1,16},{2,17},{3,18},{4,19},{5,20},{6,21},{7,22},{8,23},{9,... | collective-permute-start | bytes 860168 | tf_op jit(solution)/shard_map/ppermute | solution.py:378
  125.0 87.8 %collective-permute-start.13 = (f32[560,128]{1,0:T(8,128)}, f32[560,128]{1,0:T(8,128)S(1)}, u32[]{:S(2)}, u32[]{:S(2)}) collective-permute-start(f32[560,128]{1,0:T(8,128)} %get-tuple-element.55), channel_id=1, source_target_pairs={{0,18},{1,19},{2,20},{3,21},{4,22},{5,23},{6,24},{7,25},{8,26},{9,... | collective-permute-start | bytes 860168 | tf_op jit(solution)/shard_map/ppermute | solution.py:378
  133.8 87.1 %collective-permute-start.17 = (f32[560,128]{1,0:T(8,128)}, f32[560,128]{1,0:T(8,128)S(1)}, u32[]{:S(2)}, u32[]{:S(2)}) collective-permute-start(f32[560,128]{1,0:T(8,128)} %get-tuple-element.59), channel_id=1, source_target_pairs={{0,14},{1,15},{2,16},{3,17},{4,18},{5,19},{6,20},{7,21},{8,22},{9,... | collective-permute-start | bytes 860168 | tf_op jit(solution)/shard_map/ppermute | solution.py:378
  135.0 97.1 %collective-permute-start = (f32[560,128]{1,0:T(8,128)S(1)}, f32[560,128]{1,0:T(8,128)S(1)}, u32[]{:S(2)}, u32[]{:S(2)}) collective-permute-start(f32[560,128]{1,0:T(8,128)S(1)} %copy-done.13), channel_id=1, source_target_pairs={{0,31},{1,0},{2,1},{3,2},{4,3},{5,4},{6,5},{7,6},{8,7},{9,8},{10,9... | collective-permute-start | bytes 860168 | tf_op jit(solution)/shard_map/ppermute | solution.py:378
  207.2 26.8 %collective-permute-start.1 = (f32[560,128]{1,0:T(8,128)}, f32[560,128]{1,0:T(8,128)S(1)}, u32[]{:S(2)}, u32[]{:S(2)}) collective-permute-start(f32[560,128]{1,0:T(8,128)} %get-tuple-element.43), channel_id=1, source_target_pairs={{0,30},{1,31},{2,0},{3,1},{4,2},{5,3},{6,4},{7,5},{8,6},{9,7},{10,... | collective-permute-start | bytes 860168 | tf_op jit(solution)/shard_map/ppermute | solution.py:378
  207.2 34.2 %collective-permute-start.2 = (f32[560,128]{1,0:T(8,128)}, f32[560,128]{1,0:T(8,128)S(1)}, u32[]{:S(2)}, u32[]{:S(2)}) collective-permute-start(f32[560,128]{1,0:T(8,128)} %get-tuple-element.44), channel_id=1, source_target_pairs={{0,29},{1,30},{2,31},{3,0},{4,1},{5,2},{6,3},{7,4},{8,5},{9,6},{10... | collective-permute-start | bytes 860168 | tf_op jit(solution)/shard_map/ppermute | solution.py:378
  212.8 40.5 %collective-permute-start.3 = (f32[560,128]{1,0:T(8,128)}, f32[560,128]{1,0:T(8,128)S(1)}, u32[]{:S(2)}, u32[]{:S(2)}) collective-permute-start(f32[560,128]{1,0:T(8,128)} %get-tuple-element.45), channel_id=1, source_target_pairs={{0,28},{1,29},{2,30},{3,31},{4,0},{5,1},{6,2},{7,3},{8,4},{9,5},{1... | collective-permute-start | bytes 860168 | tf_op jit(solution)/shard_map/ppermute | solution.py:378
  220.9 47.7 %collective-permute-start.4 = (f32[560,128]{1,0:T(8,128)}, f32[560,128]{1,0:T(8,128)S(1)}, u32[]{:S(2)}, u32[]{:S(2)}) collective-permute-start(f32[560,128]{1,0:T(8,128)} %get-tuple-element.46), channel_id=1, source_target_pairs={{0,27},{1,28},{2,29},{3,30},{4,31},{5,0},{6,1},{7,2},{8,3},{9,4},{... | collective-permute-start | bytes 860168 | tf_op jit(solution)/shard_map/ppermute | solution.py:378
  232.1 55.3 %collective-permute-start.5 = (f32[560,128]{1,0:T(8,128)}, f32[560,128]{1,0:T(8,128)S(1)}, u32[]{:S(2)}, u32[]{:S(2)}) collective-permute-start(f32[560,128]{1,0:T(8,128)} %get-tuple-element.47), channel_id=1, source_target_pairs={{0,26},{1,27},{2,28},{3,29},{4,30},{5,31},{6,0},{7,1},{8,2},{9,3},... | collective-permute-start | bytes 860168 | tf_op jit(solution)/shard_map/ppermute | solution.py:378
  234.0 75.9 %collective-permute-start.6 = (f32[560,128]{1,0:T(8,128)}, f32[560,128]{1,0:T(8,128)}, u32[]{:S(2)}, u32[]{:S(2)}) collective-permute-start(f32[560,128]{1,0:T(8,128)} %get-tuple-element.48), channel_id=1, source_target_pairs={{0,25},{1,26},{2,27},{3,28},{4,29},{5,30},{6,31},{7,0},{8,1},{9,2}... | collective-permute-start | bytes 860168 | tf_op jit(solution)/shard_map/ppermute | solution.py:378
  241.4 102.0 %collective-permute-start.7 = (f32[560,128]{1,0:T(8,128)}, f32[560,128]{1,0:T(8,128)}, u32[]{:S(2)}, u32[]{:S(2)}) collective-permute-start(f32[560,128]{1,0:T(8,128)} %get-tuple-element.49), channel_id=1, source_target_pairs={{0,24},{1,25},{2,26},{3,27},{4,28},{5,29},{6,30},{7,31},{8,0},{9,1... | collective-permute-start | bytes 860168 | tf_op jit(solution)/shard_map/ppermute | solution.py:378
  253.3 109.9 %collective-permute-start.8 = (f32[560,128]{1,0:T(8,128)}, f32[560,128]{1,0:T(8,128)}, u32[]{:S(2)}, u32[]{:S(2)}) collective-permute-start(f32[560,128]{1,0:T(8,128)} %get-tuple-element.50), channel_id=1, source_target_pairs={{0,23},{1,24},{2,25},{3,26},{4,27},{5,28},{6,29},{7,30},{8,31},{9,... | collective-permute-start | bytes 860168 | tf_op jit(solution)/shard_map/ppermute | solution.py:378
  268.7 131.8 %collective-permute-start.9 = (f32[560,128]{1,0:T(8,128)}, f32[560,128]{1,0:T(8,128)}, u32[]{:S(2)}, u32[]{:S(2)}) collective-permute-start(f32[560,128]{1,0:T(8,128)} %get-tuple-element.51), channel_id=1, source_target_pairs={{0,22},{1,23},{2,24},{3,25},{4,26},{5,27},{6,28},{7,29},{8,30},{9,... | collective-permute-start | bytes 860168 | tf_op jit(solution)/shard_map/ppermute | solution.py:378
  287.4 134.0 %collective-permute-start.10 = (f32[560,128]{1,0:T(8,128)}, f32[560,128]{1,0:T(8,128)}, u32[]{:S(2)}, u32[]{:S(2)}) collective-permute-start(f32[560,128]{1,0:T(8,128)} %get-tuple-element.52), channel_id=1, source_target_pairs={{0,21},{1,22},{2,23},{3,24},{4,25},{5,26},{6,27},{7,28},{8,29},{9,... | collective-permute-start | bytes 860168 | tf_op jit(solution)/shard_map/ppermute | solution.py:378
  309.9 143.8 %collective-permute-start.11 = (f32[560,128]{1,0:T(8,128)}, f32[560,128]{1,0:T(8,128)}, u32[]{:S(2)}, u32[]{:S(2)}) collective-permute-start(f32[560,128]{1,0:T(8,128)} %get-tuple-element.53), channel_id=1, source_target_pairs={{0,20},{1,21},{2,22},{3,23},{4,24},{5,25},{6,26},{7,27},{8,28},{9,... | collective-permute-start | bytes 860168 | tf_op jit(solution)/shard_map/ppermute | solution.py:378
  343.4 161.6 %collective-permute-start.12 = (f32[560,128]{1,0:T(8,128)}, f32[560,128]{1,0:T(8,128)}, u32[]{:S(2)}, u32[]{:S(2)}) collective-permute-start(f32[560,128]{1,0:T(8,128)} %get-tuple-element.54), channel_id=1, source_target_pairs={{0,19},{1,20},{2,21},{3,22},{4,23},{5,24},{6,25},{7,26},{8,27},{9,... | collective-permute-start | bytes 860168 | tf_op jit(solution)/shard_map/ppermute | solution.py:378
  363.2 172.1 %collective-permute-start.15 = (f32[560,128]{1,0:T(8,128)}, f32[560,128]{1,0:T(8,128)}, u32[]{:S(2)}, u32[]{:S(2)}) collective-permute-start(f32[560,128]{1,0:T(8,128)} %get-tuple-element.57), channel_id=1, source_target_pairs={{0,16},{1,17},{2,18},{3,19},{4,20},{5,21},{6,22},{7,23},{8,24},{9,... | collective-permute-start | bytes 860168 | tf_op jit(solution)/shard_map/ppermute | solution.py:378
  400.5 136.0 %collective-permute-start.18 = (f32[560,128]{1,0:T(8,128)}, f32[560,128]{1,0:T(8,128)}, u32[]{:S(2)}, u32[]{:S(2)}) collective-permute-start(f32[560,128]{1,0:T(8,128)} %get-tuple-element.60), channel_id=1, source_target_pairs={{0,13},{1,14},{2,15},{3,16},{4,17},{5,18},{6,19},{7,20},{8,21},{9,... | collective-permute-start | bytes 860168 | tf_op jit(solution)/shard_map/ppermute | solution.py:378
  421.4 115.4 %collective-permute-start.19 = (f32[560,128]{1,0:T(8,128)}, f32[560,128]{1,0:T(8,128)}, u32[]{:S(2)}, u32[]{:S(2)}) collective-permute-start(f32[560,128]{1,0:T(8,128)} %get-tuple-element.61), channel_id=1, source_target_pairs={{0,12},{1,13},{2,14},{3,15},{4,16},{5,17},{6,18},{7,19},{8,20},{9,... | collective-permute-start | bytes 860168 | tf_op jit(solution)/shard_map/ppermute | solution.py:378
  453.7 86.1 %collective-permute-start.20 = (f32[560,128]{1,0:T(8,128)}, f32[560,128]{1,0:T(8,128)}, u32[]{:S(2)}, u32[]{:S(2)}) collective-permute-start(f32[560,128]{1,0:T(8,128)} %get-tuple-element.62), channel_id=1, source_target_pairs={{0,11},{1,12},{2,13},{3,14},{4,15},{5,16},{6,17},{7,18},{8,19},{9,... | collective-permute-start | bytes 860168 | tf_op jit(solution)/shard_map/ppermute | solution.py:378
  504.9 57.9 %collective-permute-start.21 = (f32[560,128]{1,0:T(8,128)}, f32[560,128]{1,0:T(8,128)}, u32[]{:S(2)}, u32[]{:S(2)}) collective-permute-start(f32[560,128]{1,0:T(8,128)} %get-tuple-element.63), channel_id=1, source_target_pairs={{0,10},{1,11},{2,12},{3,13},{4,14},{5,15},{6,16},{7,17},{8,18},{9,... | collective-permute-start | bytes 860168 | tf_op jit(solution)/shard_map/ppermute | solution.py:378
  535.3 38.4 %collective-permute-start.22 = (f32[560,128]{1,0:T(8,128)}, f32[560,128]{1,0:T(8,128)}, u32[]{:S(2)}, u32[]{:S(2)}) collective-permute-start(f32[560,128]{1,0:T(8,128)} %get-tuple-element.64), channel_id=1, source_target_pairs={{0,9},{1,10},{2,11},{3,12},{4,13},{5,14},{6,15},{7,16},{8,17},{9,1... | collective-permute-start | bytes 860168 | tf_op jit(solution)/shard_map/ppermute | solution.py:378
  536.5 66.5 %collective-permute-start.23 = (f32[560,128]{1,0:T(8,128)}, f32[560,128]{1,0:T(8,128)}, u32[]{:S(2)}, u32[]{:S(2)}) collective-permute-start(f32[560,128]{1,0:T(8,128)} %get-tuple-element.65), channel_id=1, source_target_pairs={{0,8},{1,9},{2,10},{3,11},{4,12},{5,13},{6,14},{7,15},{8,16},{9,17... | collective-permute-start | bytes 860168 | tf_op jit(solution)/shard_map/ppermute | solution.py:378
  536.8 85.4 %collective-permute-start.24 = (f32[560,128]{1,0:T(8,128)}, f32[560,128]{1,0:T(8,128)}, u32[]{:S(2)}, u32[]{:S(2)}) collective-permute-start(f32[560,128]{1,0:T(8,128)} %get-tuple-element.66), channel_id=1, source_target_pairs={{0,7},{1,8},{2,9},{3,10},{4,11},{5,12},{6,13},{7,14},{8,15},{9,16}... | collective-permute-start | bytes 860168 | tf_op jit(solution)/shard_map/ppermute | solution.py:378
  539.8 102.9 %collective-permute-start.25 = (f32[560,128]{1,0:T(8,128)}, f32[560,128]{1,0:T(8,128)}, u32[]{:S(2)}, u32[]{:S(2)}) collective-permute-start(f32[560,128]{1,0:T(8,128)} %get-tuple-element.67), channel_id=1, source_target_pairs={{0,6},{1,7},{2,8},{3,9},{4,10},{5,11},{6,12},{7,13},{8,14},{9,15},... | collective-permute-start | bytes 860168 | tf_op jit(solution)/shard_map/ppermute | solution.py:378
  562.8 98.9 %collective-permute-start.26 = (f32[560,128]{1,0:T(8,128)}, f32[560,128]{1,0:T(8,128)}, u32[]{:S(2)}, u32[]{:S(2)}) collective-permute-start(f32[560,128]{1,0:T(8,128)} %get-tuple-element.68), channel_id=1, source_target_pairs={{0,5},{1,6},{2,7},{3,8},{4,9},{5,10},{6,11},{7,12},{8,13},{9,14},{... | collective-permute-start | bytes 860168 | tf_op jit(solution)/shard_map/ppermute | solution.py:378
  573.8 88.0 %collective-permute-start.27 = (f32[560,128]{1,0:T(8,128)}, f32[560,128]{1,0:T(8,128)}, u32[]{:S(2)}, u32[]{:S(2)}) collective-permute-start(f32[560,128]{1,0:T(8,128)} %get-tuple-element.69), channel_id=1, source_target_pairs={{0,4},{1,5},{2,6},{3,7},{4,8},{5,9},{6,10},{7,11},{8,12},{9,13},{1... | collective-permute-start | bytes 860168 | tf_op jit(solution)/shard_map/ppermute | solution.py:378
  602.9 66.1 %collective-permute-start.28 = (f32[560,128]{1,0:T(8,128)}, f32[560,128]{1,0:T(8,128)}, u32[]{:S(2)}, u32[]{:S(2)}) collective-permute-start(f32[560,128]{1,0:T(8,128)} %get-tuple-element.70), channel_id=1, source_target_pairs={{0,3},{1,4},{2,5},{3,6},{4,7},{5,8},{6,9},{7,10},{8,11},{9,12},{10... | collective-permute-start | bytes 860168 | tf_op jit(solution)/shard_map/ppermute | solution.py:378
  622.1 58.6 %collective-permute-start.29 = (f32[560,128]{1,0:T(8,128)}, f32[560,128]{1,0:T(8,128)}, u32[]{:S(2)}, u32[]{:S(2)}) collective-permute-start(f32[560,128]{1,0:T(8,128)} %get-tuple-element.71), channel_id=1, source_target_pairs={{0,2},{1,3},{2,4},{3,5},{4,6},{5,7},{6,8},{7,9},{8,10},{9,11},{10,... | collective-permute-start | bytes 860168 | tf_op jit(solution)/shard_map/ppermute | solution.py:378
  642.8 42.1 %collective-permute-start.30 = (f32[560,128]{1,0:T(8,128)}, f32[560,128]{1,0:T(8,128)}, u32[]{:S(2)}, u32[]{:S(2)}) collective-permute-start(f32[560,128]{1,0:T(8,128)} %get-tuple-element.72), channel_id=1, source_target_pairs={{0,1},{1,2},{2,3},{3,4},{4,5},{5,6},{6,7},{7,8},{8,9},{9,10},{10,1... | collective-permute-start | bytes 860168 | tf_op jit(solution)/shard_map/ppermute | solution.py:378
  (16 other events, 5796.8 us)
